TPU v7x, 32 devices: a whole 2x2x4 slice. The times are simulated.
32 devices in a mesh: cp: 16 (over z, x, core), tp: 2 (over y).
Axes of the slice: x: 2, y: 2, z: 4, core: 2. Of those that a mesh axis runs over, the one named last changes fastest.
Arguments:
- hidden: bfloat16 [8192, 4096], P('cp', 'tp'), may hold values from -6 to 6
- norm_gain: float32 [4096], replicated, may hold values from 0.5 to 1.5
- w_query: bfloat16 [4096, 4096], P(None, 'tp'), may hold values from -0.140625 to 0.140625
- w_key: bfloat16 [4096, 1024], P(None, 'tp'), may hold values from -4 to 4
- w_value: bfloat16 [4096, 1024], P(None, 'tp'), may hold values from -0.09375 to 0.09375
- w_out: bfloat16 [4096, 4096], P('tp'), may hold values from -0.5 to 0.5
- doc_ids: int32 [8192], P('cp'), may hold values from 0 to 5, never falling along the last dimension, each value on 1 to 6144 neighbouring positions
Outputs:
- updated: bfloat16 [8192, 4096], P('cp', 'tp')
Inputs may be any that keep to these rules, and one draw needn't show every extreme that they name: `doc_ids`: document numbers never fall along the sequence; every document has 1 to 6144 tokens.
All inputs are finite; a program needn't handle non-finite values.
Results may differ from a plain program's by a relative error of at most 0.017.
The roundings to bfloat16 on the way count: a program that leaves them out, or rounds other values in their place, can miss the bound.
Values may be sent and summed in bfloat16 or wider, within the bound.
A program may use at most 128 MiB of HBM per device.

v0:
```python
import jax
import jax.numpy as jnp
from jax import lax
from jax.sharding import PartitionSpec as P

HEADS = 32
KV_HEADS = 8
HEAD_SIZE = 128
epsilon = 1e-05
rope_base = 500000.0


def rotate(vectors, positions):
    half = HEAD_SIZE // 2
    freqs = rope_base ** (-jnp.arange(half, dtype=jnp.float32) * 2.0 / HEAD_SIZE)
    angles = positions.astype(jnp.float32)[:, None] * freqs[None, :]
    cosine = jnp.cos(angles)[:, None, :]
    sine = jnp.sin(angles)[:, None, :]
    first = vectors[..., :half]
    second = vectors[..., half:]
    return jnp.concatenate(
        [first * cosine - second * sine, second * cosine + first * sine], axis=-1
    )


def attend_block(
    loop_state, query_matrix, query_pos, query_doc, key_matrix, value_matrix, key_pos, key_doc
):
    best, total, running_output = loop_state
    logit_matrix = jnp.einsum(
        "ucpm,ycm->cpuy", query_matrix, key_matrix, preferred_element_type=jnp.float32
    ) * HEAD_SIZE ** (-0.5)
    allowed = (key_pos[None, :] <= query_pos[:, None]) & (key_doc[None, :] == query_doc[:, None])
    masked = jnp.where(allowed, logit_matrix, jnp.float32(-1e30))
    new_best = jnp.maximum(best, jnp.max(masked, axis=-1))
    correction_scale = jnp.exp(best - new_best)
    attention_weights = jnp.where(
        allowed, jnp.exp(logit_matrix - new_best[..., None]), jnp.float32(0.0)
    )
    total = total * correction_scale + jnp.sum(attention_weights, axis=-1)
    running_output = running_output * correction_scale[..., None] + jnp.einsum(
        "sfec,csh->sfeh",
        attention_weights.astype(jnp.bfloat16),
        value_matrix,
        preferred_element_type=jnp.float32,
    )
    return (new_best, total, running_output)


def shards(hidden, norm_gain, w_query, w_key, w_value, w_out, doc_ids):
    tok_rows = hidden.shape[0]
    half_rows = tok_rows // 2
    width = norm_gain.shape[0]
    group = HEADS // KV_HEADS
    local_kv = w_key.shape[1] // HEAD_SIZE
    query_cols = w_query.shape[1]
    key_cols = w_key.shape[1]
    wide_local = hidden.astype(jnp.float32)
    squares = lax.psum(jnp.sum(wide_local * wide_local, axis=1), "tp")
    inverse_rms = lax.rsqrt(squares / width + epsilon)[:, None]
    piece = lax.all_gather(hidden, "tp", axis=1, tiled=True)
    normed_piece = (piece.astype(jnp.float32) * inverse_rms * norm_gain[None, :]).astype(
        jnp.bfloat16
    )
    projected = jnp.concatenate(
        [
            jnp.dot(normed_piece, w_query, preferred_element_type=jnp.float32),
            jnp.dot(normed_piece, w_key, preferred_element_type=jnp.float32),
            jnp.dot(normed_piece, w_value, preferred_element_type=jnp.float32),
        ],
        axis=1,
    )
    cp_rank = lax.axis_index("cp")
    positions = cp_rank * tok_rows + jnp.arange(tok_rows, dtype=jnp.int32)
    query_raw = projected[:, :query_cols].reshape(tok_rows, local_kv * group, HEAD_SIZE)
    key_raw = projected[:, query_cols : query_cols + key_cols].reshape(
        tok_rows, local_kv, HEAD_SIZE
    )
    query_matrix = (
        rotate(query_raw, positions)
        .astype(jnp.bfloat16)
        .reshape(tok_rows, local_kv, group, HEAD_SIZE)
    )
    keys_flat = rotate(key_raw, positions).astype(jnp.bfloat16).reshape(tok_rows, key_cols)
    values_flat = projected[:, query_cols + key_cols :].astype(jnp.bfloat16)
    query_doc = doc_ids.astype(jnp.float32)
    docs_flat = query_doc.astype(jnp.bfloat16)
    first_queries = query_matrix[:half_rows]
    first_pos = positions[:half_rows]
    first_doc = query_doc[:half_rows]
    second_queries = query_matrix[half_rows:]
    second_doc = query_doc[half_rows:]
    second_start = cp_rank * tok_rows + half_rows
    second_pos = second_start + jnp.arange(half_rows, dtype=jnp.int32)
    last_first = cp_rank * tok_rows + half_rows - 1
    last_second = second_start + half_rows - 1
    init_half = (
        jnp.full((local_kv, group, half_rows), -1e30, jnp.float32),
        jnp.zeros((local_kv, group, half_rows), jnp.float32),
        jnp.zeros((local_kv, group, half_rows, HEAD_SIZE), jnp.float32),
    )
    init = (init_half, init_half)
    key_piece = lax.all_gather(keys_flat, "cp", axis=0, tiled=True)
    value_piece = lax.all_gather(values_flat, "cp", axis=0, tiled=True)
    doc_piece = lax.all_gather(docs_flat, "cp", axis=0, tiled=True)
    count = key_piece.shape[0]

    def inner(index, state):
        first_state, second_state = state
        offset = index * tok_rows
        key_blk = lax.dynamic_slice_in_dim(key_piece, offset, tok_rows, 0).reshape(
            tok_rows, local_kv, HEAD_SIZE
        )
        value_blk = lax.dynamic_slice_in_dim(value_piece, offset, tok_rows, 0).reshape(
            tok_rows, local_kv, HEAD_SIZE
        )
        key_doc = lax.dynamic_slice_in_dim(doc_piece, offset, tok_rows, 0).astype(jnp.float32)
        key_pos = offset + jnp.arange(tok_rows, dtype=jnp.int32)

        def attend_first(inner_state):
            return attend_block(
                inner_state,
                first_queries,
                first_pos,
                first_doc,
                key_blk,
                value_blk,
                key_pos,
                key_doc,
            )

        def attend_second(inner_state):
            return attend_block(
                inner_state,
                second_queries,
                second_pos,
                second_doc,
                key_blk,
                value_blk,
                key_pos,
                key_doc,
            )

        first_state = lax.cond(
            offset <= last_first, attend_first, lambda inner_state: inner_state, first_state
        )
        second_state = lax.cond(
            offset <= last_second, attend_second, lambda inner_state: inner_state, second_state
        )
        return (first_state, second_state)

    final = lax.fori_loop(0, count // tok_rows, inner, init)

    def finish(state):
        result = state[2] / state[1][..., None]
        return (
            jnp.transpose(result, (2, 0, 1, 3)).reshape(half_rows, query_cols).astype(jnp.bfloat16)
        )

    attended_first = finish(final[0])
    attended_second = finish(final[1])
    attended = jnp.concatenate([attended_first, attended_second], axis=0)
    terms = jnp.dot(attended, w_out, preferred_element_type=jnp.float32)
    summed = lax.psum_scatter(terms.astype(jnp.bfloat16), "tp", scatter_dimension=1, tiled=True)
    return summed


def solution(mesh):
    in_specs = (
        P("cp", "tp"),
        P(),
        P(None, "tp"),
        P(None, "tp"),
        P(None, "tp"),
        P("tp", None),
        P("cp"),
    )
    out_specs = P("cp", "tp")
    return jax.shard_map(shards, mesh=mesh, in_specs=in_specs, out_specs=out_specs, check_vma=False)
```

profile of v0, /device:TPU:0, one launch (start us, length us, event | category | flops | bytes accessed | tf_op | source)
XLA Modules:
  0.0 622.3 jit_solution(9094426565222155319)
XLA Ops:
  7.3 2.1 multiply_reduce_fusion
  9.4 5.9 psum.7
  15.8 52.5 %all-gather.5.cloned.1.call-done = bf16[512,4096]{1,0:T(8,128)(2,1)} async-done(((bf16[512,2048]{1,0:T(8,128)(2,1)}), bf16[512,4096]{1,0:T(8,128)(2,1)}) %all-gather.5.cloned.1.call-update) | async-done | bytes 4194320 | tf_op jit(solution)/shard_map/all_gather | solution.py:61
  68.4 5.9 fusion.44
  75.4 6.6 %convolution_convert_fusion.1 = bf16[512,512]{1,0:T(8,128)(2,1)} fusion(bf16[4096,512]{1,0:T(8,128)(2,1)} %param.17, bf16[512,4096]{1,0:T(8,128)(2,1)} %all-gather.5.cloned.1.call-done, f32[4096]{0:T(1024)S(1)} %copy-done.7, f32[512]{0:T(512)S(1)} %add_rsqrt_fusion), kind=kOutput, calls=%fused_computation.61 | convolution fusion | flops 2156134400 | bytes 8931328 | tf_op jit(solution)/shard_map/dot_general | solution.py:69
  82.4 22.4 %all-gather = bf16[16,1,512]{2,1,0:T(2,128)(2,1)S(1)} all-gather(bf16[1,1,512]{2,1,0:T(2,128)(2,1)S(1)} %reshape.106), channel_id=1, replica_groups=mesh['cp'=16,'tp'=2] {'cp'}, dimensions={0}, use_global_device_ids=true | all-gather | bytes 17408 | tf_op jit(solution)/shard_map/all_gather | solution.py:105
  105.0 13.1 %convolution_bitcast_fusion = f32[64,8,16,128]{3,1,2,0:T(8,128)S(1)} fusion(bf16[4096,2048]{1,0:T(8,128)(2,1)} %param.15, bf16[512,4096]{1,0:T(8,128)(2,1)} %all-gather.5.cloned.1.call-done, f32[4096]{0:T(1024)S(1)} %copy-done.7, f32[512]{0:T(512)S(1)} %add_rsqrt_fusion), kind=kOutput, calls=%fused_computation.53 | convolution fusion | flops 8598323200 | bytes 25184256 | tf_op jit(solution)/shard_map/dot_general | solution.py:67
  119.0 1.6 add_convert_fusion
  122.3 31.2 %all-gather.7.cloned.1.call-done = bf16[8192,512]{0,1:T(8,128)(2,1)} async-done(((bf16[512,512]{0,1:T(8,128)(2,1)}), bf16[8192,512]{0,1:T(8,128)(2,1)}) %all-gather.7.cloned.1.call-update) | async-done | bytes 8388624 | tf_op jit(solution)/shard_map/all_gather | solution.py:103
  153.5 74.7 %all-gather.9.cloned.1.call-done = bf16[8192,512]{1,0:T(8,128)(2,1)} async-done(((bf16[512,512]{1,0:T(8,128)(2,1)}), bf16[8192,512]{1,0:T(8,128)(2,1)}) %all-gather.9.cloned.1.call-update) | async-done | bytes 8388624 | tf_op jit(solution)/shard_map/all_gather | solution.py:104
  229.7 1.6 broadcast_in_dim.42.clone
  231.3 68.3 %while.24 = (s32[]{:T(128)}, f32[4,4,256]{2,1,0:T(4,128)S(1)}, f32[4,4,256]{2,1,0:T(4,128)S(1)}, f32[4,4,256,128]{3,2,1,0:T(8,128)}, f32[4,4,256]{2,1,0:T(4,128)...) while((s32[]{:T(128)}, f32[4,4,256]{2,1,0:T(4,128)S(1)}, ...), condition=%wide.region_11.12_spmd.clone, body=%wide.region_2.11_spmd.clone.sunk | while | flops 2196522240 | bytes 105403112 | solution.py:152
  234.5 8.1 %conditional.6 = ((f32[4,4,256]{2,1,0:T(4,128)S(1)}, f32[4,4,256]{2,1,0:T(4,128)S(1)}, f32[4,4,256,128]{3,2,1,0:T(8,128)})) conditional(s32[]{:T(128)} %convert_element_type.128, (f32[4,4,256]{2,1,0:T(4,128)S(1)}, f32[4,4,256]{2,1,0:T(4,128)S(1)}, f32[4,4,256,128]{3,2,1,0:T(8,128)}) %tuple.72, (s32[512]{0:T(512)S(1)}, s32[256]{0:T(256)S(1)}, ...), branch_computations={%region_3.0_spmd, %region_4.6_spmd} | conditional | flops 1098260480 | bytes 51124340 | solution.py:144
  236.3 1.7 fusion.6
  238.1 3.2 multiply_add_fusion
  242.6 8.1 %conditional.7 = ((f32[4,4,256]{2,1,0:T(4,128)S(1)}, f32[4,4,256]{2,1,0:T(4,128)S(1)}, f32[4,4,256,128]{3,2,1,0:T(8,128)})) conditional(s32[]{:T(128)} %convert_element_type.129, (f32[4,4,256]{2,1,0:T(4,128)S(1)}, f32[4,4,256]{2,1,0:T(4,128)S(1)}, f32[4,4,256,128]{3,2,1,0:T(8,128)}) %tuple.74, (s32[512]{0:T(512)S(1)}, s32[]{:T(128)}, ...), branch_computations={%region_7.7_spmd, %region_8.10_spmd} | conditional | flops 1098260736 | bytes 51126392 | solution.py:147
  242.8 1.6 fusion.20
  244.4 1.7 fusion.24
  246.1 3.2 multiply_add_fusion.2
  299.6 1.9 copy.40
  301.5 2.9 copy.39
  304.4 2.1 divide_convert_fusion
  306.5 14.0 %convolution_convert_fusion = bf16[512,4096]{1,0:T(8,128)(2,1)} fusion(bf16[2048,4096]{1,0:T(8,128)(2,1)} %param.18, bf16[256,2048]{0,1:T(8,128)(2,1)S(1)} %bitcast.110, bf16[256,2048]{0,1:T(8,128)(2,1)S(1)} %bitcast.111), kind=kOutput, calls=%fused_computation.49 | convolution fusion | flops 8596226048 | bytes 23068672 | tf_op jit(solution)/shard_map/dot_general | solution.py:163
  320.5 295.2 %reduce-scatter.2.cloned.1.call-done = bf16[512,2048]{1,0:T(8,128)(2,1)} async-done(((bf16[512,4096]{1,0:T(8,128)(2,1)}), bf16[512,2048]{1,0:T(8,128)(2,1)}) %reduce-scatter.2.cloned.1.call-update) | async-done | bytes 2097168 | tf_op jit(solution)/shard_map/reduce_scatter | solution.py:164
  (184 shorter events, 63.7 us)
Async XLA Ops:
  6.5 61.8 %copy-start.7 = (f32[4096]{0:T(1024)S(1)}, f32[4096]{0:T(1024)}, u32[]{:S(2)}) copy-start(f32[4096]{0:T(1024)} %param.14) | copy-start | bytes 49156
  6.5 61.8 %all-gather.5.cloned.1.call-start = ((), (), s32[]{:S(2)}) async-start(), calls=%async_computation.1 | async-start | bytes 6291456 | tf_op jit(solution)/shard_map/all_gather | solution.py:61
  7.3 146.2 %all-gather.7.cloned.1.call-start = ((), (), s32[]{:S(2)}) async-start(), calls=%async_computation.2 | async-start | bytes 8912896 | tf_op jit(solution)/shard_map/all_gather | solution.py:103
  75.3 7.0 %copy-start.6 = (s32[512]{0:T(512)S(1)}, s32[512]{0:T(512)}, u32[]{:S(2)}) copy-start(s32[512]{0:T(512)} %param.19) | copy-start | bytes 6148
  75.4 152.8 %all-gather.9.cloned.1.call-start = ((), (), s32[]{:S(2)}) async-start(), calls=%async_computation.3 | async-start | bytes 8912896 | tf_op jit(solution)/shard_map/all_gather | solution.py:104
  82.1 533.7 %reduce-scatter.2.cloned.1.call-start = ((), (), s32[]{:S(2)}) async-start(), calls=%async_computation.4 | async-start | bytes 6291456 | tf_op jit(solution)/shard_map/reduce_scatter | solution.py:164
  236.3 1.8 copy-start
  236.3 1.8 copy-start.2
  241.2 1.3 copy-start.3
  244.4 1.8 copy-start.1
  244.4 1.8 copy-start.4
  249.3 1.3 copy-start.5
Sparse Core Ops, SparseCore 0:
  8.9 59.4 all-gather.4
  75.5 77.9 all-gather.6
  155.6 72.4 all-gather.8
  320.7 295.0 reduce-scatter.1
where the time goes:
time: 625 us; the launch traced here: 622 us
  waiting for transfers between devices  454 us (73%)
  local copies, waits for them, and re-layouts  63.1 us (10%)
  matrix products  49.1 us (8%)
  blocking collectives  28.3 us (5%)
  other arithmetic  13.6 us (2%)
  between operations  13.3 us (2%)
    reduce_scatter x1, waiting for transfers between devices, shards(): lax.psum_scatter(terms.astype(jnp.bfloat16), 'tp', scatter_dimension=1, t...  295 us
    all_gather x1, waiting for transfers between devices, shards(): value_piece = lax.all_gather(values_flat, 'cp', axis=0, tiled=True)  74.7 us
    all_gather x1, waiting for transfers between devices, shards(): piece = lax.all_gather(hidden, 'tp', axis=1, tiled=True)  52.5 us
    dynamic_slice x32, local copies, waits for them, and re-layouts, inner(): lax.dynamic_slice_in_dim(value_piece, offset, tok_rows, 0)  33.5 us
    all_gather x1, waiting for transfers between devices, shards(): key_piece = lax.all_gather(keys_flat, 'cp', axis=0, tiled=True)  31.2 us
    all_gather x1, blocking collectives, shards(): doc_piece = lax.all_gather(docs_flat, 'cp', axis=0, tiled=True)  22.4 us
    dynamic_slice x16, local copies, waits for them, and re-layouts, inner(): lax.dynamic_slice_in_dim(key_piece, offset, tok_rows, 0)  17.2 us
    dot_general x1, matrix products, shards(): terms = jnp.dot(attended, w_out, preferred_element_type=jnp.float32)  14 us
  transfers between devices with their start and end apart: 4, of which 4 were waited for; matrix products, arithmetic and copies ran while one was open for 4% of the time, Pallas kernels for 0%

commit v1 on v0

--- a/solution.py
+++ b/solution.py
@@ -101,7 +101,18 @@
     )
     init = (init_half, init_half)
     key_piece = lax.all_gather(keys_flat, "cp", axis=0, tiled=True)
-    value_piece = lax.all_gather(values_flat, "cp", axis=0, tiled=True)
+    size, here, extent = (lax.axis_size("cp"), lax.axis_index("cp"), values_flat.shape[0])
+    right = [(i, (i + 1) % size) for i in range(size)]
+    out = jnp.zeros(
+        (*values_flat.shape[:0], size * extent, *values_flat.shape[0 + 1 :]), values_flat.dtype
+    )
+    carried = values_flat
+    for step in range(size):
+        owner = (here - step) % size
+        out = lax.dynamic_update_slice_in_dim(out, carried, owner * extent, axis=0)
+        if step < size - 1:
+            carried = lax.ppermute(carried, "cp", right)
+    value_piece = out
     doc_piece = lax.all_gather(docs_flat, "cp", axis=0, tiled=True)
     count = key_piece.shape[0]
 

time: 625 us -> 680 us (1.088)
  waiting for transfers between devices: 454 us -> 496 us
  local copies, waits for them, and re-layouts: 63.1 us -> 70 us
    ppermute x0 -> x15, waiting for transfers between devices: none -> 148 us  [shards(): carried = lax.ppermute(carried, 'cp', right)]
    all_gather x1 -> x0, waiting for transfers between devices: 74.7 us -> none  [shards(): value_piece = lax.all_gather(values_flat, 'cp', axis=0, tiled=True)]
    all_gather x1, waiting for transfers between devices: 31.2 us -> 0.01 us  [shards(): key_piece = lax.all_gather(keys_flat, 'cp', axis=0, tiled=True)]
    dynamic_slice x16 -> x0, local copies, waits for them, and re-layouts: 17.2 us -> none  [inner(): lax.dynamic_slice_in_dim(key_piece, offset, tok_rows, 0)]
    ppermute x0 -> x15, local copies, waits for them, and re-layouts: none -> 16.7 us  [shards(): carried = lax.ppermute(carried, 'cp', right)]
    dynamic_update_slice x0 -> x16, local copies, waits for them, and re-layouts: none -> 13.2 us  [shards(): out = lax.dynamic_update_slice_in_dim(out, carried, owner * extent, axis=0)]
    dynamic_slice x32 -> x16, local copies, waits for them, and re-layouts: 33.5 us -> 20.4 us  [inner(): lax.dynamic_slice_in_dim(value_piece, offset, tok_rows, 0)]
  transfers between devices with their start and end apart: 4 -> 18, of which waited for: 4 -> 14; matrix products, arithmetic and copies ran while one was open for 4% -> 9% of each run, Pallas kernels for 0% -> 0%
where the time goes in v1:
time: 680 us; the launch traced here: 673 us
  waiting for transfers between devices  496 us (73%)
  local copies, waits for them, and re-layouts  70 us (10%)
  matrix products  50.4 us (7%)
  blocking collectives  26.7 us (4%)
  between operations  14.1 us (2%)
  other arithmetic  13.7 us (2%)
    reduce_scatter x1, waiting for transfers between devices, shards(): lax.psum_scatter(terms.astype(jnp.bfloat16), 'tp', scatter_dimension=1, t...  295 us
    ppermute x15, waiting for transfers between devices, shards(): carried = lax.ppermute(carried, 'cp', right)  148 us
    all_gather x1, waiting for transfers between devices, shards(): piece = lax.all_gather(hidden, 'tp', axis=1, tiled=True)  52.5 us
    all_gather x1, blocking collectives, shards(): doc_piece = lax.all_gather(docs_flat, 'cp', axis=0, tiled=True)  20.8 us
    dynamic_slice x16, local copies, waits for them, and re-layouts, inner(): lax.dynamic_slice_in_dim(value_piece, offset, tok_rows, 0)  20.4 us
    ppermute x15, local copies, waits for them, and re-layouts, shards(): carried = lax.ppermute(carried, 'cp', right)  16.7 us
    dot_general x1, matrix products, shards(): jnp.dot(normed_piece, w_query, preferred_element_type=jnp.float32)  15.1 us
    dot_general x1, matrix products, shards(): terms = jnp.dot(attended, w_out, preferred_element_type=jnp.float32)  14.1 us
  transfers between devices with their start and end apart: 18, of which 14 were waited for; matrix products, arithmetic and copies ran while one was open for 9% of the time, Pallas kernels for 0%

profile of v1, /device:TPU:0, one launch (start us, length us, event | category | flops | bytes accessed | tf_op | source)
XLA Modules:
  0.0 672.9 jit_solution(5743082728802257074)
XLA Ops:
  9.4 5.9 psum.7
  15.9 52.5 %all-gather.4.cloned.1.call-done = bf16[512,4096]{1,0:T(8,128)(2,1)} async-done(((bf16[512,2048]{1,0:T(8,128)(2,1)}), bf16[512,4096]{1,0:T(8,128)(2,1)}) %all-gather.4.cloned.1.call-update) | async-done | bytes 4194320 | tf_op jit(solution)/shard_map/all_gather | solution.py:61
  68.4 5.9 fusion.44
  75.4 5.8 convolution_convert_fusion.1
  81.3 17.0 %collective-permute-done = bf16[512,512]{1,0:T(8,128)(2,1)S(1)} collective-permute-done((bf16[512,512]{1,0:T(8,128)(2,1)S(1)}, bf16[512,512]{1,0:T(8,128)(2,1)S(1)}, u32[]{:S(2)}, u32[]{:S(2)}) %collective-permute-start) | collective-permute-done | bytes 524320 | tf_op jit(solution)/shard_map/ppermute | solution.py:114
  98.3 17.7 %collective-permute-done.1 = bf16[512,512]{1,0:T(8,128)(2,1)S(1)} collective-permute-done((bf16[512,512]{1,0:T(8,128)(2,1)S(1)}, bf16[512,512]{1,0:T(8,128)(2,1)S(1)}, u32[]{:S(2)}, u32[]{:S(2)}) %collective-permute-start.1) | collective-permute-done | bytes 524320 | tf_op jit(solution)/shard_map/ppermute | solution.py:114
  116.0 20.4 %collective-permute-done.2 = bf16[512,512]{1,0:T(8,128)(2,1)S(1)} collective-permute-done((bf16[512,512]{1,0:T(8,128)(2,1)S(1)}, bf16[512,512]{1,0:T(8,128)(2,1)S(1)}, u32[]{:S(2)}, u32[]{:S(2)}) %collective-permute-start.2) | collective-permute-done | bytes 524320 | tf_op jit(solution)/shard_map/ppermute | solution.py:114
  136.5 22.2 %collective-permute-done.3 = bf16[512,512]{1,0:T(8,128)(2,1)S(1)} collective-permute-done((bf16[512,512]{1,0:T(8,128)(2,1)S(1)}, bf16[512,512]{1,0:T(8,128)(2,1)S(1)}, u32[]{:S(2)}, u32[]{:S(2)}) %collective-permute-start.3) | collective-permute-done | bytes 524320 | tf_op jit(solution)/shard_map/ppermute | solution.py:114
  158.6 13.7 %collective-permute-done.4 = bf16[512,512]{1,0:T(8,128)(2,1)S(1)} collective-permute-done((bf16[512,512]{1,0:T(8,128)(2,1)S(1)}, bf16[512,512]{1,0:T(8,128)(2,1)S(1)}, u32[]{:S(2)}, u32[]{:S(2)}) %collective-permute-start.4) | collective-permute-done | bytes 524320 | tf_op jit(solution)/shard_map/ppermute | solution.py:114
  173.2 10.5 %collective-permute-done.5 = bf16[512,512]{1,0:T(8,128)(2,1)S(1)} collective-permute-done((bf16[512,512]{1,0:T(8,128)(2,1)S(1)}, bf16[512,512]{1,0:T(8,128)(2,1)S(1)}, u32[]{:S(2)}, u32[]{:S(2)}) %collective-permute-start.5) | collective-permute-done | bytes 524320 | tf_op jit(solution)/shard_map/ppermute | solution.py:114
  183.7 11.3 %collective-permute-done.6 = bf16[512,512]{1,0:T(8,128)(2,1)S(1)} collective-permute-done((bf16[512,512]{1,0:T(8,128)(2,1)S(1)}, bf16[512,512]{1,0:T(8,128)(2,1)S(1)}, u32[]{:S(2)}, u32[]{:S(2)}) %collective-permute-start.6) | collective-permute-done | bytes 524320 | tf_op jit(solution)/shard_map/ppermute | solution.py:114
  195.0 11.3 %collective-permute-done.7 = bf16[512,512]{1,0:T(8,128)(2,1)S(1)} collective-permute-done((bf16[512,512]{1,0:T(8,128)(2,1)S(1)}, bf16[512,512]{1,0:T(8,128)(2,1)S(1)}, u32[]{:S(2)}, u32[]{:S(2)}) %collective-permute-start.7) | collective-permute-done | bytes 524320 | tf_op jit(solution)/shard_map/ppermute | solution.py:114
  207.0 10.7 %collective-permute-done.8 = bf16[512,512]{1,0:T(8,128)(2,1)S(1)} collective-permute-done((bf16[512,512]{1,0:T(8,128)(2,1)S(1)}, bf16[512,512]{1,0:T(8,128)(2,1)S(1)}, u32[]{:S(2)}, u32[]{:S(2)}) %collective-permute-start.8) | collective-permute-done | bytes 524320 | tf_op jit(solution)/shard_map/ppermute | solution.py:114
  217.8 20.8 %all-gather = bf16[16,1,512]{2,1,0:T(2,128)(2,1)S(1)} all-gather(bf16[1,1,512]{2,1,0:T(2,128)(2,1)S(1)} %reshape.106), channel_id=1, replica_groups=mesh['cp'=16,'tp'=2] {'cp'}, dimensions={0}, use_global_device_ids=true | all-gather | bytes 17408 | tf_op jit(solution)/shard_map/all_gather | solution.py:116
  239.7 15.1 %convolution_bitcast_fusion = f32[64,8,16,128]{3,1,2,0:T(8,128)} fusion(bf16[4096,2048]{1,0:T(8,128)(2,1)} %param.15, bf16[512,4096]{1,0:T(8,128)(2,1)} %all-gather.4.cloned.1.call-done, f32[4096]{0:T(1024)S(1)} %copy-done.14, f32[512]{0:T(512)S(1)} %add_rsqrt_fusion), kind=kOutput, calls=%fused_computation.53 | convolution fusion | flops 8598323200 | bytes 25184256 | tf_op jit(solution)/shard_map/dot_general | solution.py:67
  255.0 3.1 copy.86
  260.9 8.9 %collective-permute-done.11 = bf16[512,512]{1,0:T(8,128)(2,1)} collective-permute-done((bf16[512,512]{1,0:T(8,128)(2,1)}, bf16[512,512]{1,0:T(8,128)(2,1)}, u32[]{:S(2)}, u32[]{:S(2)}) %collective-permute-start.11) | collective-permute-done | bytes 524320 | tf_op jit(solution)/shard_map/ppermute | solution.py:114
  311.7 38.9 %while.24 = (s32[]{:T(128)}, f32[4,4,256]{2,1,0:T(4,128)S(1)}, f32[4,4,256]{2,1,0:T(4,128)S(1)}, f32[4,4,256,128]{3,2,1,0:T(8,128)}, f32[4,4,256]{2,1,0:T(4,128)...) while((s32[]{:T(128)}, f32[4,4,256]{2,1,0:T(4,128)S(1)}, ...), condition=%wide.region_11.12_spmd.clone, body=%wide.region_2.11_spmd.clone.sunk | while | flops 2196522240 | bytes 100160168 | solution.py:163
  313.2 8.1 %conditional.7 = ((f32[4,4,256]{2,1,0:T(4,128)S(1)}, f32[4,4,256]{2,1,0:T(4,128)S(1)}, f32[4,4,256,128]{3,2,1,0:T(8,128)})) conditional(s32[]{:T(128)} %convert_element_type.129, (f32[4,4,256]{2,1,0:T(4,128)S(1)}, f32[4,4,256]{2,1,0:T(4,128)S(1)}, f32[4,4,256,128]{3,2,1,0:T(8,128)}) %tuple.75, (s32[512]{0:T(512)S(1)}, s32[]{:T(128)}, ...), branch_computations={%region_7.7_spmd, %region_8.10_spmd} | conditional | flops 1098260736 | bytes 49029212 | solution.py:158
  316.8 3.2 multiply_add_fusion.2
  321.3 8.0 %conditional.6 = ((f32[4,4,256]{2,1,0:T(4,128)S(1)}, f32[4,4,256]{2,1,0:T(4,128)S(1)}, f32[4,4,256,128]{3,2,1,0:T(8,128)})) conditional(s32[]{:T(128)} %convert_element_type.128, (f32[4,4,256]{2,1,0:T(4,128)S(1)}, f32[4,4,256]{2,1,0:T(4,128)S(1)}, f32[4,4,256,128]{3,2,1,0:T(8,128)}) %tuple.73, (s32[512]{0:T(512)S(1)}, s32[256]{0:T(256)S(1)}, ...), branch_computations={%region_3.3_spmd, %region_4.6_spmd} | conditional | flops 1098260480 | bytes 49027160 | solution.py:155
  324.8 3.2 multiply_add_fusion
  357.5 14.1 %convolution_convert_fusion = bf16[512,4096]{1,0:T(8,128)(2,1)} fusion(bf16[2048,4096]{1,0:T(8,128)(2,1)} %param.18, bf16[256,2048]{0,1:T(8,128)(2,1)S(1)} %bitcast.110, bf16[256,2048]{0,1:T(8,128)(2,1)S(1)} %bitcast.111), kind=kOutput, calls=%fused_computation.49 | convolution fusion | flops 8596226048 | bytes 23068672 | tf_op jit(solution)/shard_map/dot_general | solution.py:174
  371.6 294.6 %reduce-scatter.2.cloned.1.call-done = bf16[512,2048]{1,0:T(8,128)(2,1)} async-done(((bf16[512,4096]{1,0:T(8,128)(2,1)}), bf16[512,2048]{1,0:T(8,128)(2,1)}) %reduce-scatter.2.cloned.1.call-update) | async-done | bytes 2097168 | tf_op jit(solution)/shard_map/reduce_scatter | solution.py:175
  (226 shorter events, 89.8 us)
Async XLA Ops:
  6.5 61.8 %all-gather.4.cloned.1.call-start = ((), (), s32[]{:S(2)}) async-start(), calls=%async_computation.1 | async-start | bytes 6291456 | tf_op jit(solution)/shard_map/all_gather | solution.py:61
  7.3 301.3 %all-gather.6.cloned.1.call-start = ((), (), s32[]{:S(2)}) async-start(), calls=%async_computation.2 | async-start | bytes 8912896 | tf_op jit(solution)/shard_map/all_gather | solution.py:103
  15.8 59.6 %copy-start.14 = (f32[4096]{0:T(1024)S(1)}, f32[4096]{0:T(1024)}, u32[]{:S(2)}) copy-start(f32[4096]{0:T(1024)} %param.14) | copy-start | bytes 49156
  75.3 142.4 %copy-start.13 = (s32[512]{0:T(512)S(1)}, s32[512]{0:T(512)}, u32[]{:S(2)}) copy-start(s32[512]{0:T(512)} %param.19) | copy-start | bytes 6148
  75.4 590.8 %reduce-scatter.2.cloned.1.call-start = ((), (), s32[]{:S(2)}) async-start(), calls=%async_computation.3 | async-start | bytes 6291456 | tf_op jit(solution)/shard_map/reduce_scatter | solution.py:175
  81.3 17.1 %collective-permute-start = (bf16[512,512]{1,0:T(8,128)(2,1)S(1)}, bf16[512,512]{1,0:T(8,128)(2,1)S(1)}, u32[]{:S(2)}, u32[]{:S(2)}) collective-permute-start(bf16[512,512]{1,0:T(8,128)(2,1)S(1)} %convolution_convert_fusion.1), channel_id=1, source_target_pairs={{0,2},{2,4},{4,6},{6,8},{8,10},{10,12},{12,14},{14,16},{16,18},{18... | collective-permute-start | bytes 1572872 | tf_op jit(solution)/shard_map/ppermute | solution.py:114
  98.3 108.0 %copy-start.6 = (bf16[512,512]{1,0:T(8,128)(2,1)}, bf16[512,512]{1,0:T(8,128)(2,1)S(1)}, u32[]{:S(2)}) copy-start(bf16[512,512]{1,0:T(8,128)(2,1)S(1)} %collective-permute-done) | copy-start | bytes 1572868
  98.3 17.7 %collective-permute-start.1 = (bf16[512,512]{1,0:T(8,128)(2,1)S(1)}, bf16[512,512]{1,0:T(8,128)(2,1)S(1)}, u32[]{:S(2)}, u32[]{:S(2)}) collective-permute-start(bf16[512,512]{1,0:T(8,128)(2,1)S(1)} %collective-permute-done), channel_id=1, source_target_pairs={{0,2},{2,4},{4,6},{6,8},{8,10},{10,12},{12,14},{14,16},{16,18},{18... | collective-permute-start | bytes 1572872 | tf_op jit(solution)/shard_map/ppermute | solution.py:114
  116.0 90.3 %copy-start.8 = (bf16[512,512]{1,0:T(8,128)(2,1)}, bf16[512,512]{1,0:T(8,128)(2,1)S(1)}, u32[]{:S(2)}) copy-start(bf16[512,512]{1,0:T(8,128)(2,1)S(1)} %collective-permute-done.1) | copy-start | bytes 1572868
  116.0 20.5 %collective-permute-start.2 = (bf16[512,512]{1,0:T(8,128)(2,1)S(1)}, bf16[512,512]{1,0:T(8,128)(2,1)S(1)}, u32[]{:S(2)}, u32[]{:S(2)}) collective-permute-start(bf16[512,512]{1,0:T(8,128)(2,1)S(1)} %collective-permute-done.1), channel_id=1, source_target_pairs={{0,2},{2,4},{4,6},{6,8},{8,10},{10,12},{12,14},{14,16},{16,18},{18... | collective-permute-start | bytes 1572872 | tf_op jit(solution)/shard_map/ppermute | solution.py:114
  136.4 69.8 %copy-start.10 = (bf16[512,512]{1,0:T(8,128)(2,1)}, bf16[512,512]{1,0:T(8,128)(2,1)S(1)}, u32[]{:S(2)}) copy-start(bf16[512,512]{1,0:T(8,128)(2,1)S(1)} %collective-permute-done.2) | copy-start | bytes 1572868
  136.5 22.2 %collective-permute-start.3 = (bf16[512,512]{1,0:T(8,128)(2,1)S(1)}, bf16[512,512]{1,0:T(8,128)(2,1)S(1)}, u32[]{:S(2)}, u32[]{:S(2)}) collective-permute-start(bf16[512,512]{1,0:T(8,128)(2,1)S(1)} %collective-permute-done.2), channel_id=1, source_target_pairs={{0,2},{2,4},{4,6},{6,8},{8,10},{10,12},{12,14},{14,16},{16,18},{18... | collective-permute-start | bytes 1572872 | tf_op jit(solution)/shard_map/ppermute | solution.py:114
  158.6 13.7 %collective-permute-start.4 = (bf16[512,512]{1,0:T(8,128)(2,1)S(1)}, bf16[512,512]{1,0:T(8,128)(2,1)S(1)}, u32[]{:S(2)}, u32[]{:S(2)}) collective-permute-start(bf16[512,512]{1,0:T(8,128)(2,1)S(1)} %collective-permute-done.3), channel_id=1, source_target_pairs={{0,2},{2,4},{4,6},{6,8},{8,10},{10,12},{12,14},{14,16},{16,18},{18... | collective-permute-start | bytes 1572872 | tf_op jit(solution)/shard_map/ppermute | solution.py:114
  172.4 11.3 %collective-permute-start.5 = (bf16[512,512]{1,0:T(8,128)(2,1)S(1)}, bf16[512,512]{1,0:T(8,128)(2,1)S(1)}, u32[]{:S(2)}, u32[]{:S(2)}) collective-permute-start(bf16[512,512]{1,0:T(8,128)(2,1)S(1)} %collective-permute-done.4), channel_id=1, source_target_pairs={{0,2},{2,4},{4,6},{6,8},{8,10},{10,12},{12,14},{14,16},{16,18},{18... | collective-permute-start | bytes 1572872 | tf_op jit(solution)/shard_map/ppermute | solution.py:114
  183.7 11.3 %collective-permute-start.6 = (bf16[512,512]{1,0:T(8,128)(2,1)S(1)}, bf16[512,512]{1,0:T(8,128)(2,1)S(1)}, u32[]{:S(2)}, u32[]{:S(2)}) collective-permute-start(bf16[512,512]{1,0:T(8,128)(2,1)S(1)} %collective-permute-done.5), channel_id=1, source_target_pairs={{0,2},{2,4},{4,6},{6,8},{8,10},{10,12},{12,14},{14,16},{16,18},{18... | collective-permute-start | bytes 1572872 | tf_op jit(solution)/shard_map/ppermute | solution.py:114
  195.0 11.3 %collective-permute-start.7 = (bf16[512,512]{1,0:T(8,128)(2,1)S(1)}, bf16[512,512]{1,0:T(8,128)(2,1)S(1)}, u32[]{:S(2)}, u32[]{:S(2)}) collective-permute-start(bf16[512,512]{1,0:T(8,128)(2,1)S(1)} %collective-permute-done.6), channel_id=1, source_target_pairs={{0,2},{2,4},{4,6},{6,8},{8,10},{10,12},{12,14},{14,16},{16,18},{18... | collective-permute-start | bytes 1572872 | tf_op jit(solution)/shard_map/ppermute | solution.py:114
  206.3 48.5 %copy-start.7 = (bf16[512,512]{1,0:T(8,128)(2,1)}, bf16[512,512]{1,0:T(8,128)(2,1)S(1)}, u32[]{:S(2)}) copy-start(bf16[512,512]{1,0:T(8,128)(2,1)S(1)} %collective-permute-done.7) | copy-start | bytes 1572868
  206.3 11.4 %collective-permute-start.8 = (bf16[512,512]{1,0:T(8,128)(2,1)S(1)}, bf16[512,512]{1,0:T(8,128)(2,1)S(1)}, u32[]{:S(2)}, u32[]{:S(2)}) collective-permute-start(bf16[512,512]{1,0:T(8,128)(2,1)S(1)} %collective-permute-done.7), channel_id=1, source_target_pairs={{0,2},{2,4},{4,6},{6,8},{8,10},{10,12},{12,14},{14,16},{16,18},{18... | collective-permute-start | bytes 1572872 | tf_op jit(solution)/shard_map/ppermute | solution.py:114
  217.7 21.1 %collective-permute-start.9 = (bf16[512,512]{1,0:T(8,128)(2,1)S(1)}, bf16[512,512]{1,0:T(8,128)(2,1)}, u32[]{:S(2)}, u32[]{:S(2)}) collective-permute-start(bf16[512,512]{1,0:T(8,128)(2,1)S(1)} %collective-permute-done.8), channel_id=1, source_target_pairs={{0,2},{2,4},{4,6},{6,8},{8,10},{10,12},{12,14},{14,16},{16,18},{18... | collective-permute-start | bytes 1572872 | tf_op jit(solution)/shard_map/ppermute | solution.py:114
  238.8 19.3 %collective-permute-start.10 = (bf16[512,512]{1,0:T(8,128)(2,1)}, bf16[512,512]{1,0:T(8,128)(2,1)}, u32[]{:S(2)}, u32[]{:S(2)}) collective-permute-start(bf16[512,512]{1,0:T(8,128)(2,1)} %collective-permute-done.9), channel_id=1, source_target_pairs={{0,2},{2,4},{4,6},{6,8},{8,10},{10,12},{12,14},{14,16},{16,18},{18... | collective-permute-start | bytes 1572872 | tf_op jit(solution)/shard_map/ppermute | solution.py:114
  258.1 11.7 %collective-permute-start.11 = (bf16[512,512]{1,0:T(8,128)(2,1)}, bf16[512,512]{1,0:T(8,128)(2,1)}, u32[]{:S(2)}, u32[]{:S(2)}) collective-permute-start(bf16[512,512]{1,0:T(8,128)(2,1)} %collective-permute-done.10), channel_id=1, source_target_pairs={{0,2},{2,4},{4,6},{6,8},{8,10},{10,12},{12,14},{14,16},{16,18},{18... | collective-permute-start | bytes 1572872 | tf_op jit(solution)/shard_map/ppermute | solution.py:114
  269.8 14.4 %collective-permute-start.12 = (bf16[512,512]{1,0:T(8,128)(2,1)}, bf16[512,512]{1,0:T(8,128)(2,1)}, u32[]{:S(2)}, u32[]{:S(2)}) collective-permute-start(bf16[512,512]{1,0:T(8,128)(2,1)} %collective-permute-done.11), channel_id=1, source_target_pairs={{0,2},{2,4},{4,6},{6,8},{8,10},{10,12},{12,14},{14,16},{16,18},{18... | collective-permute-start | bytes 1572872 | tf_op jit(solution)/shard_map/ppermute | solution.py:114
  284.2 11.7 %collective-permute-start.13 = (bf16[512,512]{1,0:T(8,128)(2,1)}, bf16[512,512]{1,0:T(8,128)(2,1)}, u32[]{:S(2)}, u32[]{:S(2)}) collective-permute-start(bf16[512,512]{1,0:T(8,128)(2,1)} %collective-permute-done.12), channel_id=1, source_target_pairs={{0,2},{2,4},{4,6},{6,8},{8,10},{10,12},{12,14},{14,16},{16,18},{18... | collective-permute-start | bytes 1572872 | tf_op jit(solution)/shard_map/ppermute | solution.py:114
  295.9 11.5 %collective-permute-start.14 = (bf16[512,512]{1,0:T(8,128)(2,1)}, bf16[512,512]{1,0:T(8,128)(2,1)S(1)}, u32[]{:S(2)}, u32[]{:S(2)}) collective-permute-start(bf16[512,512]{1,0:T(8,128)(2,1)} %collective-permute-done.13), channel_id=1, source_target_pairs={{0,2},{2,4},{4,6},{6,8},{8,10},{10,12},{12,14},{14,16},{16,18},{18... | collective-permute-start | bytes 1572872 | tf_op jit(solution)/shard_map/ppermute | solution.py:114
  (9 other events, 109.8 us)
Sparse Core Ops, SparseCore 0:
  8.9 59.4 all-gather.3
  75.5 90.2 all-gather.5
  371.7 294.4 reduce-scatter.1
